TPU v7x, 32 devices: a whole 2x2x4 slice. The times are simulated.
32 devices in a mesh: gx: 2 (over x), gy: 4 (over y, core), gz: 4 (over z).
Axes of the slice: x: 2, y: 2, z: 4, core: 2. Of those that a mesh axis runs over, the one named last changes fastest.
Arguments:
- charges: bfloat16 [8, 16, 16, 32, 128], P('gx', 'gy', 'gz'), may hold values from -6 to 6
- counts: int32 [8, 16, 16], P('gx', 'gy', 'gz'), may hold values from 32 to 128, as said below
- near_offsets: int32 [27, 3], replicated, may hold values from -1 to 1, as said below
- near_blocks: bfloat16 [27, 128, 128], replicated, may hold values from -0.109375 to 0.109375
- leaf_basis: bfloat16 [48, 128], replicated, may hold values from -0.5 to 0.5
- transfer: bfloat16 [8, 48, 48], replicated, may hold values from -0.625 to 0.625
- far_offsets: int32 [2, 32, 3], replicated, may hold values from -2 to 2, as said below
- coupling: bfloat16 [2, 32, 48, 48], replicated, may hold values from -0.15625 to 0.15625
- coarse_coupling: bfloat16 [2, 4, 4, 48, 48], replicated, may hold values from -0.3125 to 0.3125
Outputs:
- potentials: float32 [8, 16, 16, 32, 128], P('gx', 'gy', 'gz')
Inputs may be any that keep to these rules, and one draw needn't show every extreme that they name: `counts`: in each device's block of 4 x 4 x 4 leaf boxes some box holds 128 points. `near_offsets`: each of the 27 offsets with components in -1, 0, 1 appears once. `far_offsets`: each level lists 32 distinct offsets whose largest component in magnitude is 2.
All inputs are finite; a program needn't handle non-finite values.
Results may differ from a plain program's by a relative error of at most 0.008.
Values may be sent and summed in bfloat16 or wider, within the bound.
A program may use at most 128 MiB of HBM per device.

v0:
```python
import functools

import jax
import jax.numpy as jnp
from jax import lax
from jax.experimental import pallas as pl
from jax.experimental.pallas import tpu as pltpu
from jax.sharding import PartitionSpec as P

MESH = pl.DeviceIdType.MESH
AXES = ("gx", "gy", "gz")
F32 = jnp.float32
BF16 = jnp.bfloat16
NT = (((1,), (1,)), ((), ()))
NN = (((1,), (0,)), ((), ()))


def dot(a, b, dims):
    return lax.dot_general(a, b, dims, preferred_element_type=F32)


def kernel(
    sizes,
    near_offsets,
    counts,
    far_offsets,
    charges,
    basis,
    transfer,
    near_hbm,
    coupling_hbm,
    coarse_hbm,
    out,
    ext,
    mom,
    one,
    two,
    near_w,
    coupling_raw,
    coarse_raw,
    far_w,
    coarse_w,
    trans_w,
    basis_w,
    near_acc,
    far_acc,
    one_acc,
    code,
    inverse,
    local_sem,
    send_sem,
    recv_sem,
    gsend,
    grecv,
):
    bx, by, bz, rhs, pts = charges.shape
    rank = basis.shape[0]
    half = rhs // 2
    lane = pts // 2
    me = [lax.axis_index(a) for a in AXES]
    steps = coupling_raw.shape[1]
    cells = sizes[0] * sizes[1] * sizes[2]

    near_copy = pltpu.make_async_copy(near_hbm, near_w, local_sem.at[0])
    coupling_copy = pltpu.make_async_copy(coupling_hbm, coupling_raw, local_sem.at[1])
    coarse_copy = pltpu.make_async_copy(coarse_hbm, coarse_raw, local_sem.at[2])
    near_copy.start()
    coupling_copy.start()
    coarse_copy.start()

    barrier = pltpu.get_barrier_semaphore()
    peers = 0
    for axis in range(3):
        for d in range(1, sizes[axis]):
            other = lax.rem(me[axis] + d, sizes[axis])
            pl.semaphore_signal(barrier, inc=1, device_id={AXES[axis]: other}, device_id_type=MESH)
            peers += 1

    lanes = lax.broadcasted_iota(jnp.int32, (rhs, pts), 1)

    def mask_box(b, carry):
        x, y, z = b // (by * bz), b // bz % by, b % bz
        value = charges[x, y, z]
        live = (lanes < counts[x, y, z]).astype(F32).astype(BF16)
        ext[1 + x, 1 + y, 1 + z] = value * live
        return carry

    lax.fori_loop(0, bx * by * bz, mask_box, 0)

    def halo(ref, stream, width, order):
        own = [(bx, by, bz), (bx, by, bz), (bx // 2, by // 2, bz // 2)][stream]
        high = [ref.shape[d] == own[d] + 2 * width for d in range(3)]
        part = {
            "o": lambda d: pl.ds(width, own[d]),
            "l": lambda d: pl.ds(0, width),
            "h": lambda d: pl.ds(width + own[d], width),
            "f": lambda d: pl.ds(0, ref.shape[d]),
        }
        first, second, third = order
        plans = [("A", first, {}), ("B", second, {first: "o"})]
        plans += [("Bs", second, {first: side}) for side in "lh"]
        plans += [("C", third, {first: "o", second: "o"})]
        plans += [("Cs", third, {first: side, second: "o"}) for side in "lh"]
        plans += [("Cf", third, {first: "f", second: side}) for side in "lh"]
        groups = {"A": [], "B": [], "Bs": [], "C": [], "Cs": [], "Cf": []}
        slot = stream * 18
        for name, axis, fixed in plans:
            if any(side == "h" and not high[d] for d, side in fixed.items()):
                continue

            def view(start):
                index = [part[fixed.get(d, "o")](d) for d in range(3)]
                index[axis] = pl.ds(start, width)
                return ref.at[tuple(index)]

            n = own[axis]
            moves = [(n, 0, 1)]
            if high[axis]:
                moves.append((width, width + n, sizes[axis] - 1))
            for src, dst, shift in moves:
                groups[name].append(
                    pltpu.make_async_remote_copy(
                        src_ref=view(src),
                        dst_ref=view(dst),
                        send_sem=send_sem.at[slot],
                        recv_sem=recv_sem.at[slot],
                        device_id={AXES[axis]: lax.rem(me[axis] + shift, sizes[axis])},
                        device_id_type=MESH,
                    )
                )
                slot += 1
        return groups

    def gather(axis):
        index = [pl.ds(0, sizes[d]) if d < axis else pl.ds(me[d], 1) for d in range(3)]
        view = two.at[tuple(index)]
        copies = []
        base = sum(sizes[d] - 1 for d in range(axis))
        for d in range(1, sizes[axis]):
            copies.append(
                pltpu.make_async_remote_copy(
                    src_ref=view,
                    dst_ref=view,
                    send_sem=gsend.at[base + d - 1],
                    recv_sem=grecv.at[base + d - 1],
                    device_id={AXES[axis]: lax.rem(me[axis] + d, sizes[axis])},
                    device_id_type=MESH,
                )
            )
        return copies

    def start(copies):
        for c in copies:
            c.start()

    def arrive(copies):
        for c in copies:
            c.wait_recv()

    def gather_arrive(axis):
        base = sum(sizes[d] - 1 for d in range(axis))
        for d in range(1, sizes[axis]):
            source = lax.rem(me[axis] + sizes[axis] - d, sizes[axis])
            index = [pl.ds(0, sizes[k]) if k < axis else pl.ds(me[k], 1) for k in range(3)]
            index[axis] = pl.ds(source, 1)
            view = two.at[tuple(index)]
            pltpu.make_async_remote_copy(
                src_ref=view,
                dst_ref=view,
                send_sem=gsend.at[base + d - 1],
                recv_sem=grecv.at[base + d - 1],
                device_id={AXES[axis]: source},
                device_id_type=MESH,
            ).wait_recv()

    ch = halo(ext, 0, 1, (0, 1, 2))
    mo = halo(mom, 1, 2, (0, 2, 1))
    on = halo(one, 2, 2, (0, 1, 2))
    tw = [gather(a) for a in range(3)]

    def begin(groups):
        for name in ("A", "B", "C"):
            start(groups[name])

    def middle(groups):
        for k, copy in enumerate(groups["A"]):
            copy.wait_recv()
            start(groups["Bs"][2 * k : 2 * k + 2])
            start(groups["Cs"][2 * k : 2 * k + 2])

    def corner(groups):
        for k in range(2):
            arrive(groups["B"][k::2])
            arrive(groups["Bs"][k::2])
            start(groups["Cf"][2 * k : 2 * k + 2])

    def ending(groups):
        for name in ("C", "Cs", "Cf"):
            arrive(groups[name])

    basis_w[...] = jnp.zeros(basis_w.shape, BF16)
    basis_w[0:rank, 0:pts] = basis[...]
    basis_w[lane : lane + rank, pts : 2 * pts] = basis[...]
    trans_w[...] = jnp.zeros(trans_w.shape, BF16)
    for c in range(8):
        trans_w[c, 0:rank, 0:rank] = transfer[c]
        trans_w[c, lane : lane + rank, lane : lane + rank] = transfer[c]

    def moments(x, carry):
        low = ext[1 + x, 1 : 1 + by, 1 : 1 + bz, 0:half].reshape(by * bz * half, pts)
        high = ext[1 + x, 1 : 1 + by, 1 : 1 + bz, half:rhs].reshape(by * bz * half, pts)
        value = dot(jnp.concatenate([low, high], axis=1), basis_w[...], NT).astype(BF16)
        mom[2 + x, 2 : 2 + by, 2 : 2 + bz] = value.reshape(by, bz, half, pts)
        return carry

    lax.fori_loop(0, bx, moments, 0)
    pl.semaphore_wait(barrier, peers)
    begin(mo)

    hx, hy, hz = bx // 2, by // 2, bz // 2
    parents = [(a, b, c) for a in range(hx) for b in range(hy) for c in range(hz)]
    kids = [(i, j, l) for i in range(2) for j in range(2) for l in range(2)]
    total = jnp.zeros((len(parents) * half, pts), F32)
    for number, (i, j, l) in enumerate(kids):
        rows = jnp.concatenate(
            [mom[2 + 2 * a + i, 2 + 2 * b + j, 2 + 2 * c + l] for a, b, c in parents], axis=0
        )
        total = total + dot(rows, trans_w[number], NT)
    value = total.astype(BF16)
    for n, (a, b, c) in enumerate(parents):
        one[2 + a, 2 + b, 2 + c] = value[n * half : (n + 1) * half]
    begin(on)
    total = jnp.zeros((half, pts), F32)
    for number in range(8):
        total = total + dot(value[number * half : (number + 1) * half], trans_w[number], NT)
    two[me[0], me[1], me[2]] = total.astype(BF16)
    start(tw[0])
    begin(ch)

    stencil = near_offsets.shape[1]
    for number in range(stencil):
        x, y, z = (near_offsets[d, number] + 1 for d in range(3))
        code[number] = x * 9 + y * 3 + z

    def invert(c, carry):
        found = jnp.int32(0)
        for number in range(stencil):
            found = found + jnp.where(code[number] == c, number, 0)
        inverse[c] = jnp.minimum(found, stencil - 1)
        return carry

    lax.fori_loop(0, stencil, invert, 0)
    far_w[...] = jnp.zeros(far_w.shape, BF16)
    coarse_w[...] = jnp.zeros(coarse_w.shape, BF16)
    coupling_copy.wait()

    def build_far(t, carry):
        for level in range(2):
            for k in range(4):
                value = coupling_raw[level, 4 * t + k]
                for s in range(2):
                    col = k * pts + s * lane
                    far_w[level, t, s * lane : s * lane + rank, col : col + rank] = value
        return carry

    lax.fori_loop(0, steps // 4, build_far, 0)

    middle(mo)
    middle(on)
    gather_arrive(0)
    start(tw[1])

    coarse_copy.wait()

    def build_coarse(t, carry):
        for k in range(2):
            r = 2 * t + k
            x, y, z = r // (sizes[1] * sizes[2]), r // sizes[2] % sizes[1], r % sizes[2]
            value = coarse_raw[x, y, z]
            for s in range(2):
                col = k * pts + s * lane
                coarse_w[t, s * lane : s * lane + rank, col : col + rank] = value
        return carry

    lax.fori_loop(0, cells // 2, build_coarse, 0)
    near_copy.wait()

    def window(ox, oy, oz):
        v = ext[pl.ds(ox + 1, bx), pl.ds(oy + 1, by), pl.ds(oz + 1, bz)]
        return v.reshape(bx * by * bz * rhs, pts)

    def near_weight(ox, oy, oz):
        return near_w[inverse[(ox + 1) * 9 + (oy + 1) * 3 + oz + 1]]

    near_acc[...] = dot(window(0, 0, 0), near_weight(0, 0, 0), NT)

    def near_pair(first, second):
        rows = jnp.concatenate([window(*first), window(*second)], axis=1)
        mats = jnp.concatenate([near_weight(*first), near_weight(*second)], axis=1)
        near_acc[...] += dot(rows, mats, NT)

    gather_arrive(1)
    start(tw[2])
    corner(on)
    corner(mo)
    middle(ch)
    near_pair((-1, 0, 0), (1, 0, 0))
    corner(ch)

    def near_middle(t, carry):
        near_pair((t - 1, -1, 0), (t - 1, 1, 0))
        return carry

    lax.fori_loop(0, 3, near_middle, 0)

    gather_arrive(2)

    def coarse_step(t, total):
        rows = []
        for k in range(2):
            r = 2 * t + k
            x, y, z = r // (sizes[1] * sizes[2]), r // sizes[2] % sizes[1], r % sizes[2]
            rows.append(
                two[
                    lax.rem(me[0] + x, sizes[0]),
                    lax.rem(me[1] + y, sizes[1]),
                    lax.rem(me[2] + z, sizes[2]),
                ]
            )
        return total + dot(jnp.concatenate(rows, axis=1), coarse_w[t], NT)

    local_two = lax.fori_loop(0, cells // 2, coarse_step, jnp.zeros((half, pts), F32))

    ending(on)

    def far_window(ref, level, e, count):
        ox, oy, oz = (far_offsets[d, level, e] + 2 for d in range(3))
        planes = []
        for i in range(count[0]):
            x = lax.rem(ox + i, ref.shape[0])
            v = ref[x, pl.ds(oy, count[1]), pl.ds(oz, count[2])]
            planes.append(v.reshape(count[1] * count[2] * half, pts))
        return jnp.concatenate(planes, axis=0)

    def far_product(ref, level, t, count):
        rows = [far_window(ref, level, 4 * t + k, count) for k in range(4)]
        return dot(jnp.concatenate(rows, axis=1), far_w[level, t], NT)

    one_acc[...] = jnp.zeros(one_acc.shape, F32)

    def far_one(t, carry):
        one_acc[...] += far_product(one, 1, t, (hx, hy, hz))
        return carry

    lax.fori_loop(0, steps // 4, far_one, 0)

    rounded = local_two.astype(BF16)
    for number in range(8):
        rows = slice(number * half, (number + 1) * half)
        one_acc[rows, :] += dot(rounded, trans_w[number], NN)

    rounded = one_acc[...].astype(BF16)
    for number, (i, j, l) in enumerate(kids):
        value = dot(rounded, trans_w[number], NN)
        for n, (a, b, c) in enumerate(parents):
            box = ((2 * a + i) * by + 2 * b + j) * bz + 2 * c + l
            far_acc[box * half : (box + 1) * half, :] = value[n * half : (n + 1) * half]

    arrive(ch["C"])
    arrive(ch["Cs"])

    def near_side(t, carry):
        near_pair((t - 1, 0, -1), (t - 1, 0, 1))
        return carry

    lax.fori_loop(0, 3, near_side, 0)

    ending(mo)

    def far_zero(t, carry):
        far_acc[...] += far_product(mom, 0, t, (bx, by, bz))
        return carry

    lax.fori_loop(0, steps // 4, far_zero, 0)

    arrive(ch["Cf"])

    def near_corner(t, carry):
        x, y = t // 2 - 1, t % 2 * 2 - 1
        near_pair((x, y, -1), (x, y, 1))
        return carry

    lax.fori_loop(0, 6, near_corner, 0)

    def finish(x, carry):
        span = by * bz * half
        rows = far_acc[pl.ds(pl.multiple_of(x * span, span), span), :].astype(BF16)
        value = dot(rows, basis_w[...], NN)
        for b in range(by * bz):
            y, z = b // bz, b % bz
            live = (lanes < counts[x, y, z]).astype(F32)
            far = jnp.concatenate(
                [
                    value[b * half : (b + 1) * half, 0:pts],
                    value[b * half : (b + 1) * half, pts : 2 * pts],
                ],
                axis=0,
            )
            at = pl.multiple_of((x * by * bz + b) * rhs, rhs)
            out[x, y, z] = (near_acc[pl.ds(at, rhs), :] + far) * live
        return carry

    lax.fori_loop(0, bx, finish, 0)

    groups = list(ch.values()) + list(mo.values()) + list(on.values()) + tw
    for group in groups:
        for c in group:
            c.wait_send()


def body(
    sizes,
    charges,
    counts,
    near_offsets,
    near_blocks,
    leaf_basis,
    transfer,
    far_offsets,
    coupling,
    coarse_coupling,
):
    bx, by, bz, rhs, pts = charges.shape
    half = rhs // 2
    stencil = near_offsets.shape[0]
    boxes = bx * by * bz
    hx, hy, hz = bx // 2, by // 2, bz // 2
    one_x = hx + 2 if sizes[0] * hx == hx + 2 else hx + 4
    levels, steps = coupling.shape[:2]
    cells = sizes[0] * sizes[1] * sizes[2]
    peers = sum(sizes) - 3
    smem = pl.BlockSpec(memory_space=pltpu.SMEM)
    vmem = pl.BlockSpec(memory_space=pltpu.VMEM)
    hbm = pl.BlockSpec(memory_space=pl.ANY)
    return pl.pallas_call(
        functools.partial(kernel, sizes),
        out_shape=jax.ShapeDtypeStruct(charges.shape, F32),
        in_specs=[smem, smem, smem, vmem, vmem, vmem, hbm, hbm, hbm],
        out_specs=vmem,
        scratch_shapes=[
            pltpu.VMEM((bx + 2, by + 2, bz + 2, rhs, pts), BF16),
            pltpu.VMEM((bx + 4, by + 4, bz + 4, half, pts), BF16),
            pltpu.VMEM((one_x, hy + 4, hz + 4, half, pts), BF16),
            pltpu.VMEM(tuple(sizes) + (half, pts), BF16),
            pltpu.VMEM(near_blocks.shape, BF16),
            pltpu.VMEM(coupling.shape, BF16),
            pltpu.VMEM(coarse_coupling.shape, BF16),
            pltpu.VMEM((levels, steps // 4, pts, 4 * pts), BF16),
            pltpu.VMEM((cells // 2, pts, 2 * pts), BF16),
            pltpu.VMEM((8, pts, pts), BF16),
            pltpu.VMEM((pts, 2 * pts), BF16),
            pltpu.VMEM((boxes * rhs, pts), F32),
            pltpu.VMEM((boxes * half, pts), F32),
            pltpu.VMEM((hx * hy * hz * half, pts), F32),
            pltpu.SMEM((stencil,), jnp.int32),
            pltpu.SMEM((stencil,), jnp.int32),
            pltpu.SemaphoreType.DMA((3,)),
            pltpu.SemaphoreType.DMA((54,)),
            pltpu.SemaphoreType.DMA((54,)),
            pltpu.SemaphoreType.DMA((peers,)),
            pltpu.SemaphoreType.DMA((peers,)),
        ],
        compiler_params=pltpu.CompilerParams(
            collective_id=0, has_side_effects=True, vmem_limit_bytes=56 * 1024 * 1024
        ),
    )(
        near_offsets.T,
        counts,
        far_offsets.transpose(2, 0, 1),
        charges,
        leaf_basis,
        transfer,
        near_blocks,
        coupling,
        coarse_coupling,
    )


def solution(mesh):
    sizes = tuple(mesh.shape[a] for a in AXES)
    in_specs = (
        P("gx", "gy", "gz", None, None),
        P("gx", "gy", "gz"),
        P(),
        P(),
        P(),
        P(),
        P(),
        P(),
        P(),
    )
    out_specs = P("gx", "gy", "gz", None, None)
    return jax.shard_map(
        functools.partial(body, sizes),
        mesh=mesh,
        in_specs=in_specs,
        out_specs=out_specs,
        check_vma=False,
    )
```

profile of v0, /device:TPU:1, one launch (start us, length us, event | category | flops | bytes accessed | tf_op | source)
XLA Modules:
  0.0 52.4 jit_solution(1986450943998083055)
XLA Ops:
  0.0 50.1 %shard_map.91 = f32[4,4,4,32,128]{4,3,2,1,0:T(8,128)} custom-call(s32[3,27]{1,0:T(4,128)} %bitcast.3, s32[4,4,4]{2,1,0:T(4,128)} %counts.1, s32[3,2,32]{2,1,0:T(2,128)} %bitcast.2, bf16[4,4,4,32,128]{4,3,2,1,0:T(8,128)(2,1)} %charges.1, bf16[48,128]{1,0:T(8,128)(2,1)} %basis.1, bf16[8,48,48]{2,1,0:T(8,128)(2,1)} %transfer.1, bf16[27,128,128]{2,1,0:T(8,128)(2,1)} %near_hbm.1, ...), custom_call_target="tpu_custom_call" | custom-call | tf_op jit(solution)/shard_map/pallas_call | solution.py:445
  50.1 2.3 %copy.11 = f32[4,4,4,32,128]{4,3,2,1,0:T(8,128)} copy(f32[4,4,4,32,128]{4,3,2,1,0:T(8,128)} %shard_map.91) | data formatting | bytes 2097152
where the time goes:
time: 52.6 us; the launch traced here: 52.4 us
  Pallas kernels  50.1 us (95%)
  local copies, waits for them, and re-layouts  2.29 us (4%)
    pallas_call x1, Pallas kernels, body(): pl.pallas_call(functools.partial(kernel, sizes), out_shape=jax.ShapeDtype...  50.1 us
    unnamed x1, local copies, waits for them, and re-layouts  2.29 us

commit v1 on v0

v1 whole, which is shorter than its diff:
```python
import functools

import jax
import jax.numpy as jnp
from jax import lax
from jax.experimental import pallas as pl
from jax.experimental.pallas import tpu as pltpu
from jax.sharding import PartitionSpec as P

MESH = pl.DeviceIdType.MESH
AXES = ("gx", "gy", "gz")
F32 = jnp.float32
BF16 = jnp.bfloat16
NT = (((1,), (1,)), ((), ()))
NN = (((1,), (0,)), ((), ()))


def dot(a, b, dims):
    return lax.dot_general(a, b, dims, preferred_element_type=F32)


def kernel(
    sizes,
    near_offsets,
    counts,
    far_offsets,
    charges_hbm,
    basis,
    transfer,
    near_hbm,
    coupling_hbm,
    coarse_hbm,
    out,
    charges,
    ext,
    mom,
    one,
    two,
    near_w,
    coupling_raw,
    coarse_raw,
    far_w,
    coarse_w,
    trans_w,
    basis_w,
    near_acc,
    far_acc,
    one_acc,
    inverse,
    local_sem,
    send_sem,
    recv_sem,
    gsend,
    grecv,
):
    bx, by, bz, rhs, pts = charges.shape
    rank = basis.shape[0]
    half = rhs // 2
    lane = pts // 2
    me = [lax.axis_index(a) for a in AXES]
    steps = coupling_raw.shape[1]
    cells = sizes[0] * sizes[1] * sizes[2]
    hx, hy, hz = bx // 2, by // 2, bz // 2

    charges_copy = pltpu.make_async_copy(charges_hbm, charges, local_sem.at[3])
    near_copy = pltpu.make_async_copy(near_hbm, near_w, local_sem.at[0])
    coupling_copy = pltpu.make_async_copy(coupling_hbm, coupling_raw, local_sem.at[1])
    coarse_copy = pltpu.make_async_copy(coarse_hbm, coarse_raw, local_sem.at[2])
    charges_copy.start()
    near_copy.start()
    coupling_copy.start()
    coarse_copy.start()

    barrier = pltpu.get_barrier_semaphore()
    peers = 0
    for axis in range(3):
        for d in range(1, sizes[axis]):
            other = lax.rem(me[axis] + d, sizes[axis])
            pl.semaphore_signal(barrier, inc=1, device_id={AXES[axis]: other}, device_id_type=MESH)
            peers += 1

    slots = [0]

    def halo(ref, own, width, order):
        high = [ref.shape[d] == own[d] + 2 * width for d in range(3)]
        sides = ["lh" if high[d] else "l" for d in range(3)]
        part = {
            "o": lambda d: pl.ds(width, own[d]),
            "l": lambda d: pl.ds(0, width),
            "h": lambda d: pl.ds(width + own[d], width),
        }
        first, second, third = order

        def moves(axis, fixed):
            def view(start):
                index = [part[fixed.get(d, "o")](d) for d in range(3)]
                index[axis] = pl.ds(start, width)
                return ref.at[tuple(index)]

            n = own[axis]
            pairs = [(n, 0, 1)]
            if high[axis]:
                pairs.append((width, width + n, sizes[axis] - 1))
            copies = []
            for src, dst, shift in pairs:
                slot = slots[0]
                slots[0] += 1
                copies.append(
                    pltpu.make_async_remote_copy(
                        src_ref=view(src),
                        dst_ref=view(dst),
                        send_sem=send_sem.at[slot],
                        recv_sem=recv_sem.at[slot],
                        device_id={AXES[axis]: lax.rem(me[axis] + shift, sizes[axis])},
                        device_id_type=MESH,
                    )
                )
            return copies

        groups = {"A": moves(first, {}), "B": moves(second, {}), "C": moves(third, {})}
        groups["AB"] = [moves(second, {first: a}) for a in sides[first]]
        groups["AC"] = [moves(third, {first: a}) for a in sides[first]]
        groups["BC"] = [moves(third, {second: b}) for b in sides[second]]
        groups["ABC"] = [
            [moves(third, {first: a, second: b}) for b in sides[second]] for a in sides[first]
        ]
        return groups

    def flat(items):
        if isinstance(items, (list, tuple)):
            return [c for item in items for c in flat(item)]
        return [items]

    def start(items):
        for c in flat(items):
            c.start()

    def arrive(items):
        for c in flat(items):
            c.wait_recv()

    def got_first(groups):
        for k, copy in enumerate(groups["A"]):
            copy.wait_recv()
            start(groups["AB"][k])
            start(groups["AC"][k])

    def got_second(groups):
        for k, copy in enumerate(groups["B"]):
            copy.wait_recv()
            start(groups["BC"][k])

    def got_edge(groups):
        for a, copies in enumerate(groups["AB"]):
            for b, copy in enumerate(copies):
                copy.wait_recv()
                start(groups["ABC"][a][b])

    ring = (2, 0, 1)

    def gather(stage):
        axis = ring[stage]
        done = ring[:stage]
        base = sum(sizes[d] - 1 for d in done)

        def view(place):
            index = [pl.ds(0, sizes[d]) if d in done else pl.ds(me[d], 1) for d in range(3)]
            index[axis] = pl.ds(place, 1)
            return two.at[tuple(index)]

        sends, receives = [], []
        for d in range(1, sizes[axis]):
            for place, other, copies in (
                (me[axis], lax.rem(me[axis] + d, sizes[axis]), sends),
                (lax.rem(me[axis] + sizes[axis] - d, sizes[axis]), None, receives),
            ):
                copies.append(
                    pltpu.make_async_remote_copy(
                        src_ref=view(place),
                        dst_ref=view(place),
                        send_sem=gsend.at[base + d - 1],
                        recv_sem=grecv.at[base + d - 1],
                        device_id={AXES[axis]: place if other is None else other},
                        device_id_type=MESH,
                    )
                )
        return sends, receives

    ch = halo(ext, (bx, by, bz), 1, (0, 2, 1))
    mo = halo(mom, (bx, by, bz), 2, (2, 0, 1))
    on = halo(one, (hx, hy, hz), 2, (0, 2, 1))
    tw = [gather(k) for k in range(3)]

    basis_w[...] = jnp.zeros(basis_w.shape, BF16)
    basis_w[0:rank, 0:pts] = basis[...]
    basis_w[lane : lane + rank, pts : 2 * pts] = basis[...]
    trans_w[...] = jnp.zeros(trans_w.shape, BF16)
    for c in range(8):
        trans_w[c, 0:rank, 0:rank] = transfer[c]
        trans_w[c, lane : lane + rank, lane : lane + rank] = transfer[c]
    far_w[...] = jnp.zeros(far_w.shape, BF16)

    lanes = lax.broadcasted_iota(jnp.int32, (half, pts), 1)
    charges_copy.wait()

    def mask_row(b, carry):
        x, y = b // by, b % by
        for z in range(bz):
            live = (lanes < counts[x, y, z]).astype(F32).astype(BF16)
            live = jnp.concatenate([live, live], axis=0)
            ext[1 + x, 1 + y, 1 + z] = charges[x, y, z] * live
        return carry

    lax.fori_loop(0, bx * by, mask_row, 0)
    pl.semaphore_wait(barrier, peers)
    start(ch["A"])
    start(ch["C"])

    def moments(x, carry):
        low = ext[1 + x, 1 : 1 + by, 1 : 1 + bz, 0:half].reshape(by * bz * half, pts)
        high = ext[1 + x, 1 : 1 + by, 1 : 1 + bz, half:rhs].reshape(by * bz * half, pts)
        value = dot(jnp.concatenate([low, high], axis=1), basis_w[...], NT).astype(BF16)
        mom[2 + x, 2 : 2 + by, 2 : 2 + bz] = value.reshape(by, bz, half, pts)
        return carry

    lax.fori_loop(0, bx, moments, 0)
    start(mo["A"])
    start(mo["C"])

    parents = [(a, b, c) for a in range(hx) for b in range(hy) for c in range(hz)]
    kids = [(i, j, l) for i in range(2) for j in range(2) for l in range(2)]
    total = jnp.zeros((len(parents) * half, pts), F32)
    for number, (i, j, l) in enumerate(kids):
        rows = jnp.concatenate(
            [mom[2 + 2 * a + i, 2 + 2 * b + j, 2 + 2 * c + l] for a, b, c in parents], axis=0
        )
        total = total + dot(rows, trans_w[number], NT)
    value = total.astype(BF16)
    for n, (a, b, c) in enumerate(parents):
        one[2 + a, 2 + b, 2 + c] = value[n * half : (n + 1) * half]
    start(on["A"])
    start(mo["B"])
    start(on["B"])
    start(on["C"])
    total = jnp.zeros((half, pts), F32)
    for number in range(8):
        total = total + dot(value[number * half : (number + 1) * half], trans_w[number], NT)
    two[me[0], me[1], me[2]] = total.astype(BF16)
    start(tw[0][0])
    start(ch["B"])

    stencil = near_offsets.shape[1]
    codes = []
    for number in range(stencil):
        x, y, z = (near_offsets[d, number] + 1 for d in range(3))
        codes.append(x * 9 + y * 3 + z)

    def invert(c, carry):
        found = jnp.int32(0)
        for number in range(stencil):
            found = found + jnp.where(codes[number] == c, number, 0)
        inverse[c] = jnp.minimum(found, stencil - 1)
        return carry

    lax.fori_loop(0, stencil, invert, 0)
    coupling_copy.wait()

    def build_far(t, carry):
        for level in range(2):
            for k in range(4):
                value = coupling_raw[level, 4 * t + k]
                for s in range(2):
                    col = k * pts + s * lane
                    far_w[level, t, s * lane : s * lane + rank, col : col + rank] = value
        return carry

    lax.fori_loop(0, steps // 4, build_far, 0)
    near_copy.wait()

    blank = jnp.zeros((pts, pts), BF16)

    def near_rows(dx, dz):
        columns = []
        for k in range(4):
            planes = [
                ext[pl.ds(1 + dx, bx), 2 * j + k, pl.ds(1 + dz, bz)].reshape(bx * bz * rhs, pts)
                for j in range(by // 2)
            ]
            columns.append(jnp.concatenate(planes, axis=0))
        return columns

    def near_weights(dx, dz):
        blocks = [near_w[inverse[(dx + 1) * 9 + k * 3 + dz + 1]] for k in range(3)]
        return blocks + [blank], [blank] + blocks

    def near_product(places):
        rows, even, odd = [], [], []
        for dx, dz in places:
            rows += near_rows(dx, dz)
            first, second = near_weights(dx, dz)
            even += first
            odd += second
        mats = jnp.concatenate(
            [jnp.concatenate(even, axis=1), jnp.concatenate(odd, axis=1)], axis=0
        )
        return dot(jnp.concatenate(rows, axis=1), mats, NT)

    arrive(ch["C"])
    near_acc[...] = near_product([(0, 0)])

    got_first(ch)
    got_first(on)
    got_first(mo)
    arrive(tw[0][1])
    start(tw[1][0])

    coarse_w[...] = jnp.zeros(coarse_w.shape, BF16)
    coarse_copy.wait()

    def build_coarse(t, carry):
        for k in range(2):
            r = 2 * t + k
            x, y, z = r // (sizes[1] * sizes[2]), r // sizes[2] % sizes[1], r % sizes[2]
            value = coarse_raw[x, y, z]
            for s in range(2):
                col = k * pts + s * lane
                coarse_w[t, s * lane : s * lane + rank, col : col + rank] = value
        return carry

    lax.fori_loop(0, cells // 2, build_coarse, 0)

    got_second(on)
    arrive(ch["AC"])
    near_acc[...] += near_product([(-1, 0), (1, 0)])
    arrive(tw[1][1])
    start(tw[2][0])
    got_second(mo)
    got_edge(on)
    got_second(ch)
    got_edge(mo)
    got_edge(ch)
    arrive(tw[2][1])

    group = 16

    def coarse_step(u, total):
        rows, mats = [], []
        for k in range(group):
            t = u * group + k
            for r in (2 * t, 2 * t + 1):
                x, y, z = r // (sizes[1] * sizes[2]), r // sizes[2] % sizes[1], r % sizes[2]
                rows.append(
                    two[
                        lax.rem(me[0] + x, sizes[0]),
                        lax.rem(me[1] + y, sizes[1]),
                        lax.rem(me[2] + z, sizes[2]),
                    ]
                )
            mats.append(coarse_w[t])
        return total + dot(jnp.concatenate(rows, axis=1), jnp.concatenate(mats, axis=1), NT)

    local_two = lax.fori_loop(
        0, cells // 2 // group, coarse_step, jnp.zeros((half, pts), F32)
    )

    arrive([on["C"], on["AC"], on["BC"], on["ABC"]])

    def far_window(ref, level, e, count):
        ox, oy, oz = (far_offsets[d, level, e] + 2 for d in range(3))
        planes = []
        for i in range(count[0]):
            x = lax.rem(ox + i, ref.shape[0])
            v = ref[x, pl.ds(oy, count[1]), pl.ds(oz, count[2])]
            planes.append(v.reshape(count[1] * count[2] * half, pts))
        return jnp.concatenate(planes, axis=0)

    def far_product(ref, level, t, many, count):
        rows = [far_window(ref, level, 4 * t + k, count) for k in range(4 * many)]
        mats = [far_w[level, t + k] for k in range(many)]
        return dot(jnp.concatenate(rows, axis=1), jnp.concatenate(mats, axis=1), NT)

    one_acc[...] = jnp.zeros(one_acc.shape, F32)

    def far_one(t, carry):
        one_acc[...] += far_product(one, 1, 4 * t, 4, (hx, hy, hz))
        return carry

    lax.fori_loop(0, steps // 16, far_one, 0)

    rounded = local_two.astype(BF16)
    for number in range(8):
        rows = slice(number * half, (number + 1) * half)
        one_acc[rows, :] += dot(rounded, trans_w[number], NN)

    rounded = one_acc[...].astype(BF16)
    for number, (i, j, l) in enumerate(kids):
        value = dot(rounded, trans_w[number], NN)
        for n, (a, b, c) in enumerate(parents):
            box = ((2 * a + i) * by + 2 * b + j) * bz + 2 * c + l
            far_acc[box * half : (box + 1) * half, :] = value[n * half : (n + 1) * half]

    arrive(ch["BC"])
    near_acc[...] += near_product([(0, -1), (0, 1)])

    arrive([mo["C"], mo["AC"], mo["BC"], mo["ABC"]])

    def far_zero(t, carry):
        far_acc[...] += far_product(mom, 0, 2 * t, 2, (bx, by, bz))
        return carry

    lax.fori_loop(0, steps // 8, far_zero, 0)

    arrive(ch["ABC"])

    def near_corner(t, carry):
        near_acc[...] += near_product([(2 * t - 1, -1), (2 * t - 1, 1)])
        return carry

    lax.fori_loop(0, 2, near_corner, 0)

    def finish(x, carry):
        span = by * bz * half
        rows = far_acc[pl.ds(pl.multiple_of(x * span, span), span), :].astype(BF16)
        value = dot(rows, basis_w[...], NN)
        for b in range(by * bz):
            y, z = b // bz, b % bz
            live = (lanes < counts[x, y, z]).astype(F32)
            live = jnp.concatenate([live, live], axis=0)
            far = jnp.concatenate(
                [
                    value[b * half : (b + 1) * half, 0:pts],
                    value[b * half : (b + 1) * half, pts : 2 * pts],
                ],
                axis=0,
            )
            at = pl.multiple_of(((y // 2 * bx + x) * bz + z) * rhs, rhs)
            col = y % 2 * pts
            out[x, y, z] = (near_acc[pl.ds(at, rhs), col : col + pts] + far) * live
        return carry

    lax.fori_loop(0, bx, finish, 0)

    for groups in (ch, mo, on):
        for c in flat(list(groups.values())):
            c.wait_send()
    for sends, receives in tw:
        for c in sends:
            c.wait_send()


def body(
    sizes,
    charges,
    counts,
    near_offsets,
    near_blocks,
    leaf_basis,
    transfer,
    far_offsets,
    coupling,
    coarse_coupling,
):
    bx, by, bz, rhs, pts = charges.shape
    half = rhs // 2
    stencil = near_offsets.shape[0]
    boxes = bx * by * bz
    hx, hy, hz = bx // 2, by // 2, bz // 2
    one_x = hx + 2 if sizes[0] * hx == hx + 2 else hx + 4
    levels, steps = coupling.shape[:2]
    cells = sizes[0] * sizes[1] * sizes[2]
    peers = sum(sizes) - 3
    smem = pl.BlockSpec(memory_space=pltpu.SMEM)
    vmem = pl.BlockSpec(memory_space=pltpu.VMEM)
    hbm = pl.BlockSpec(memory_space=pl.ANY)
    return pl.pallas_call(
        functools.partial(kernel, sizes),
        out_shape=pltpu.VMEM(charges.shape, F32),
        in_specs=[smem, smem, smem, hbm, vmem, vmem, hbm, hbm, hbm],
        out_specs=vmem,
        scratch_shapes=[
            pltpu.VMEM(charges.shape, BF16),
            pltpu.VMEM((bx + 2, by + 2, bz + 2, rhs, pts), BF16),
            pltpu.VMEM((bx + 4, by + 4, bz + 4, half, pts), BF16),
            pltpu.VMEM((one_x, hy + 4, hz + 4, half, pts), BF16),
            pltpu.VMEM(tuple(sizes) + (half, pts), BF16),
            pltpu.VMEM(near_blocks.shape, BF16),
            pltpu.VMEM(coupling.shape, BF16),
            pltpu.VMEM(coarse_coupling.shape, BF16),
            pltpu.VMEM((levels, steps // 4, pts, 4 * pts), BF16),
            pltpu.VMEM((cells // 2, pts, 2 * pts), BF16),
            pltpu.VMEM((8, pts, pts), BF16),
            pltpu.VMEM((pts, 2 * pts), BF16),
            pltpu.VMEM((boxes // 2 * rhs, 2 * pts), F32),
            pltpu.VMEM((boxes * half, pts), F32),
            pltpu.VMEM((hx * hy * hz * half, pts), F32),
            pltpu.SMEM((stencil,), jnp.int32),
            pltpu.SemaphoreType.DMA((4,)),
            pltpu.SemaphoreType.DMA((78,)),
            pltpu.SemaphoreType.DMA((78,)),
            pltpu.SemaphoreType.DMA((peers,)),
            pltpu.SemaphoreType.DMA((peers,)),
        ],
        compiler_params=pltpu.CompilerParams(
            collective_id=0, has_side_effects=True, vmem_limit_bytes=56 * 1024 * 1024
        ),
    )(
        near_offsets.T,
        counts,
        far_offsets.transpose(2, 0, 1),
        charges,
        leaf_basis,
        transfer,
        near_blocks,
        coupling,
        coarse_coupling,
    )


def solution(mesh):
    sizes = tuple(mesh.shape[a] for a in AXES)
    in_specs = (
        P("gx", "gy", "gz", None, None),
        P("gx", "gy", "gz"),
        P(),
        P(),
        P(),
        P(),
        P(),
        P(),
        P(),
    )
    out_specs = P("gx", "gy", "gz", None, None)
    return jax.shard_map(
        functools.partial(body, sizes),
        mesh=mesh,
        in_specs=in_specs,
        out_specs=out_specs,
        check_vma=False,
    )
```

time: 52.6 us -> 44.6 us (0.85)
  Pallas kernels: 50.1 us -> 43.5 us
  local copies, waits for them, and re-layouts: 2.29 us -> 0.97 us
    pallas_call x1, Pallas kernels: 50.1 us -> 43.5 us  [body(): pl.pallas_call(functools.partial(kernel, sizes), out_shape=pltpu.VMEM(cha...]
    unnamed x1, local copies, waits for them, and re-layouts: 2.29 us -> 0.97 us
where the time goes in v1:
time: 44.6 us; the launch traced here: 44.4 us
  Pallas kernels  43.5 us (98%)
  local copies, waits for them, and re-layouts  0.97 us (2%)
    pallas_call x1, Pallas kernels, body(): pl.pallas_call(functools.partial(kernel, sizes), out_shape=pltpu.VMEM(cha...  43.5 us
    unnamed x1, local copies, waits for them, and re-layouts  0.97 us

profile of v1, /device:TPU:1, one launch (start us, length us, event | category | flops | bytes accessed | tf_op | source)
XLA Modules:
  0.0 44.4 jit_solution(1122420645198812804)
XLA Ops:
  0.0 43.5 %shard_map.91 = f32[4,4,4,32,128]{4,3,2,1,0:T(8,128)S(1)} custom-call(s32[3,27]{1,0:T(4,128)} %bitcast.3, s32[4,4,4]{2,1,0:T(4,128)} %counts.1, s32[3,2,32]{2,1,0:T(2,128)} %bitcast.2, bf16[4,4,4,32,128]{4,3,2,1,0:T(8,128)(2,1)} %charges_hbm.1, bf16[48,128]{1,0:T(8,128)(2,1)} %basis.1, bf16[8,48,48]{2,1,0:T(8,128)(2,1)} %transfer.1, ...), custom_call_target="tpu_custom_call" | custom-call | tf_op jit(solution)/shard_map/pallas_call | solution.py:475
  43.5 1.0 %copy.11 = f32[4,4,4,32,128]{4,3,2,1,0:T(8,128)} copy(f32[4,4,4,32,128]{4,3,2,1,0:T(8,128)S(1)} %shard_map.91) | data formatting | bytes 2097152

commit v2 on v1

v2 whole, which is shorter than its diff:
```python
import functools

import jax
import jax.numpy as jnp
from jax import lax
from jax.experimental import pallas as pl
from jax.experimental.pallas import tpu as pltpu
from jax.sharding import PartitionSpec as P

MESH = pl.DeviceIdType.MESH
AXES = ("gx", "gy", "gz")
F32 = jnp.float32
BF16 = jnp.bfloat16
NT = (((1,), (1,)), ((), ()))
NN = (((1,), (0,)), ((), ()))


def dot(a, b, dims):
    return lax.dot_general(a, b, dims, preferred_element_type=F32)


def kernel(
    sizes,
    near_offsets_hbm,
    counts_hbm,
    far_offsets_hbm,
    charges_hbm,
    basis_hbm,
    transfer_hbm,
    near_hbm,
    coupling_hbm,
    coarse_hbm,
    out,
    near_offsets,
    counts,
    far_offsets,
    charges,
    basis,
    transfer,
    ext,
    mom,
    one,
    two,
    near_w,
    coupling_raw,
    coarse_raw,
    far_w,
    coarse_w,
    trans_w,
    basis_w,
    spread,
    near_acc,
    far_acc,
    one_acc,
    span,
    inverse,
    local_sem,
    send_sem,
    recv_sem,
):
    bx, by, bz, rhs, pts = charges.shape
    rank = basis.shape[0]
    half = rhs // 2
    lane = pts // 2
    me = [lax.axis_index(a) for a in AXES]
    steps = coupling_raw.shape[1]
    cells = sizes[0] * sizes[1] * sizes[2]
    hx, hy, hz = bx // 2, by // 2, bz // 2

    pairs = (
        (counts_hbm, counts),
        (charges_hbm, charges),
        (basis_hbm, basis),
        (transfer_hbm, transfer),
        (near_offsets_hbm, near_offsets),
        (far_offsets_hbm, far_offsets),
        (near_hbm, near_w),
        (coupling_hbm, coupling_raw),
        (coarse_hbm, coarse_raw),
    )
    local = [
        pltpu.make_async_copy(src, dst, local_sem.at[n]) for n, (src, dst) in enumerate(pairs)
    ]
    for copy in local:
        copy.start()

    barrier = pltpu.get_barrier_semaphore()
    peers = 0
    for axis in range(3):
        for d in range(1, sizes[axis]):
            other = lax.rem(me[axis] + d, sizes[axis])
            pl.semaphore_signal(barrier, inc=1, device_id={AXES[axis]: other}, device_id_type=MESH)
            peers += 1

    slots = [0]
    sent = [0]

    def tiles_of(ref):
        count = 1
        for n in ref.shape:
            count *= n
        return count // (half * pts)

    class Batch:
        def __init__(self):
            self.sem = recv_sem.at[slots[0]]
            slots[0] += 1
            self.copies = []
            self.tiles = 0

        def add(self, src, dst, device):
            self.copies.append(
                pltpu.make_async_remote_copy(
                    src_ref=src,
                    dst_ref=dst,
                    send_sem=send_sem.at[0],
                    recv_sem=self.sem,
                    device_id=device,
                    device_id_type=MESH,
                )
            )
            self.tiles += tiles_of(dst)

        def start(self, only=None):
            for c in self.copies if only is None else self.copies[only]:
                c.start()
            if only is None:
                sent[0] += self.tiles

        def wait(self):
            drain(self.sem, self.tiles)

    def drain(sem, tiles):
        while tiles > 0:
            n = min(tiles, span.shape[0])
            view = span.at[pl.ds(0, n)]
            pltpu.make_async_copy(view, view, sem).wait()
            tiles -= n

    def halo(ref, own, width, order, packed):
        extent = [ref.shape[d] for d in ((0, 2, 4) if packed else (0, 1, 2))]
        high = [extent[d] == own[d] + 2 * width[d] for d in range(3)]
        sides = ["lh" if high[d] else "l" for d in range(3)]
        part = {
            "o": lambda d: pl.ds(width[d], own[d]),
            "l": lambda d: pl.ds(0, width[d]),
            "h": lambda d: pl.ds(width[d] + own[d], width[d]),
        }
        first, second, third = order

        def moves(batch, axis, fixed, only="lh"):
            def views(start):
                index = [part[fixed.get(d, "o")](d) for d in range(3)]
                index[axis] = pl.ds(start, w)
                if not packed:
                    return [ref.at[tuple(index)]]
                return [
                    ref.at[index[0], i, index[1], pl.ds(0, 2 - i), index[2]] for i in range(2)
                ]

            n, w = own[axis], width[axis]
            if "l" in only:
                target = {AXES[axis]: lax.rem(me[axis] + 1, sizes[axis])}
                for src, dst in zip(views(n), views(0)):
                    batch.add(src, dst, target)
            if "h" in only and high[axis]:
                target = {AXES[axis]: lax.rem(me[axis] + sizes[axis] - 1, sizes[axis])}
                for src, dst in zip(views(w), views(w + n)):
                    batch.add(src, dst, target)
            return batch

        groups = {"A": [moves(Batch(), first, {}, side) for side in sides[first]]}
        groups["B"] = moves(Batch(), second, {})
        groups["AB"] = Batch()
        for a in sides[first]:
            moves(groups["AB"], second, {first: a})
        last = [Batch() for k in range(1 if packed else 4)]
        cuts = []
        for k, places in enumerate(
            (
                [{}],
                [{first: a} for a in sides[first]],
                [{second: b} for b in sides[second]],
                [{first: a, second: b} for a in sides[first] for b in sides[second]],
            )
        ):
            batch = last[0] if packed else last[k]
            begin = len(batch.copies)
            for fixed in places:
                moves(batch, third, fixed)
            cuts.append((batch, begin, len(batch.copies)))
        groups["last"] = last
        for batch in last:
            sent[0] += batch.tiles

        def send(k, low=0, high=None):
            batch, begin, end = cuts[k]
            n = end - begin
            high = n if high is None else high
            batch.start(slice(begin + low, begin + high))

        groups["send"] = send
        groups["per"] = len(cuts[0][0].copies[: cuts[0][2]])
        return groups

    def got_first(groups):
        per_second = len(groups["B"].copies)
        per_third = groups["per"]
        for k, batch in enumerate(groups["A"]):
            batch.wait()
            groups["AB"].start(slice(k * per_second, (k + 1) * per_second))
            groups["send"](1, k * per_third, (k + 1) * per_third)
        sent[0] += groups["AB"].tiles

    def got_second(groups):
        groups["B"].wait()
        groups["send"](2)

    def got_edge(groups):
        groups["AB"].wait()
        groups["send"](3)

    ring = (2, 1, 0)

    def gather(stage):
        axis = ring[stage]
        done = ring[:stage]
        batch = Batch()

        index = [pl.ds(0, sizes[d]) if d in done else pl.ds(me[d], 1) for d in range(3)]
        view = two.at[tuple(index)]
        for d in range(1, sizes[axis]):
            batch.add(view, view, {AXES[axis]: lax.rem(me[axis] + d, sizes[axis])})
        return batch

    parts = spread.shape[1] // pts
    third = rank // parts
    ch = halo(ext, (bx, by, bz), (1, 1, 1), (0, 2, 1), False)
    mo = halo(mom, (hx, hy, bz), (1, 1, 2), (2, 0, 1), True)
    on = halo(one, (hx // 2, hy // 2, hz), (1, 1, 2), (0, 2, 1), True)
    tw = [gather(k) for k in range(3)]

    local[2].wait()
    local[3].wait()
    basis_w[...] = jnp.zeros(basis_w.shape, BF16)
    basis_w[0:rank, 0:pts] = basis[...]
    basis_w[lane : lane + rank, pts : 2 * pts] = basis[...]
    trans_w[...] = jnp.zeros(trans_w.shape, BF16)
    for c in range(8):
        trans_w[c, 0:rank, 0:rank] = transfer[c]
        trans_w[c, lane : lane + rank, lane : lane + rank] = transfer[c]
    far_w[...] = jnp.zeros(far_w.shape, BF16)
    target = lax.broadcasted_iota(jnp.int32, (pts, pts), 0)
    source = lax.broadcasted_iota(jnp.int32, (pts, pts), 1)
    moved = jnp.where(source % lane >= rank, source - rank, -pts)
    for q in range(parts):
        hit = (target == moved + q * third).astype(F32).astype(BF16)
        spread[:, q * pts : (q + 1) * pts] = hit

    def pack(last):
        return dot(last, spread[...], NN).astype(BF16)

    def unpack(tiles):
        return dot(jnp.concatenate(tiles, axis=1), spread[...], NT).astype(BF16)

    lanes = lax.broadcasted_iota(jnp.int32, (half, pts), 1)
    local[0].wait()
    local[1].wait()

    def mask_row(b, carry):
        x, y = b // by, b % by
        for z in range(bz):
            live = (lanes < counts[x, y, z]).astype(F32).astype(BF16)
            live = jnp.concatenate([live, live], axis=0)
            ext[1 + x, 1 + y, 1 + z] = charges[x, y, z] * live
        return carry

    lax.fori_loop(0, bx * by, mask_row, 0)
    pl.semaphore_wait(barrier, peers)
    for batch in ch["A"]:
        batch.start()
    ch["send"](0)

    values = []
    for x in range(bx):
        low = ext[1 + x, 1 : 1 + by, 1 : 1 + bz, 0:half].reshape(by * bz * half, pts)
        high = ext[1 + x, 1 : 1 + by, 1 : 1 + bz, half:rhs].reshape(by * bz * half, pts)
        value = dot(jnp.concatenate([low, high], axis=1), basis_w[...], NT).astype(BF16)
        values.append(value.reshape(hy, 2, bz * half, pts))
    for a in range(hx):
        for b in range(hy):
            tiles = [values[2 * a + q // 2][b, q % 2] for q in range(parts + 1)]
            extra = pack(tiles[parts])
            for q in range(parts + 1):
                tile = tiles[q]
                if q < parts:
                    tile = tile + extra[:, q * pts : (q + 1) * pts]
                mom[1 + a, q // 2, 1 + b, q % 2, 2 : 2 + bz] = tile.reshape(bz, half, pts)
    for batch in mo["A"]:
        batch.start()
    mo["send"](0)
    mo["B"].start()
    ch["B"].start()

    parents = [(a, b, c) for a in range(hx) for b in range(hy) for c in range(hz)]
    kids = [(i, j, l) for i in range(2) for j in range(2) for l in range(2)]
    total = jnp.zeros((len(parents) * half, pts), F32)
    for number, (i, j, l) in enumerate(kids):
        rows = jnp.concatenate(
            [mom[1 + a, i, 1 + b, j, 2 + 2 * c + l] for a, b, c in parents], axis=0
        )
        total = total + dot(rows, trans_w[number], NT)
    value = total.astype(BF16)
    pieces = {p: value[n * half : (n + 1) * half] for n, p in enumerate(parents)}
    for a in range(hx // 2):
        for b in range(hy // 2):
            tiles = [
                jnp.concatenate([pieces[2 * a + i, 2 * b + j, c] for c in range(hz)], axis=0)
                for i in range(2)
                for j in range(2)
            ]
            extra = pack(tiles[parts])
            for q in range(parts + 1):
                tile = tiles[q]
                if q < parts:
                    tile = tile + extra[:, q * pts : (q + 1) * pts]
                one[1 + a, q // 2, 1 + b, q % 2, 2 : 2 + hz] = tile.reshape(hz, half, pts)
    total = jnp.zeros((half, pts), F32)
    for number in range(8):
        total = total + dot(value[number * half : (number + 1) * half], trans_w[number], NT)
    two[me[0], me[1], me[2]] = total.astype(BF16)
    for batch in on["A"]:
        batch.start()
    tw[0].start()
    on["B"].start()
    on["send"](0)

    local[4].wait()
    local[5].wait()
    stencil = near_offsets.shape[1]
    words = [jnp.int32(0)] * 9
    for number in range(stencil):
        x, y, z = (near_offsets[d, number] + 1 for d in range(3))
        key = x * 3 + y
        value = jnp.where(z == 0, number, jnp.where(z == 1, number * 32, number * 1024))
        words = [w + jnp.where(key == k, value, 0) for k, w in enumerate(words)]
    for k in range(9):
        inverse[k] = words[k]
    local[7].wait()

    def build_far(t, carry):
        for level in range(2):
            for u in range(2):
                for k in range(4):
                    value = coupling_raw[level, 8 * t + 4 * u + k]
                    for s in range(2):
                        col = k * pts + s * lane
                        far_w[level, 2 * t + u, s * lane : s * lane + rank, col : col + rank] = value
        return carry

    lax.fori_loop(0, steps // 8, build_far, 0)
    local[6].wait()

    blank = jnp.zeros((pts, pts), BF16)

    def near_rows(dx, dz):
        columns = []
        for k in range(4):
            planes = [
                ext[pl.ds(1 + dx, bx), 2 * j + k, pl.ds(1 + dz, bz)].reshape(bx * bz * rhs, pts)
                for j in range(by // 2)
            ]
            columns.append(jnp.concatenate(planes, axis=0))
        return columns

    def near_weights(dx, dz):
        blocks = []
        for k in range(3):
            found = (inverse[(dx + 1) * 3 + k] // 32 ** (dz + 1)) % 32
            blocks.append(near_w[jnp.minimum(found, near_w.shape[0] - 1)])
        return blocks + [blank], [blank] + blocks

    def near_product(places):
        rows, even, odd = [], [], []
        for dx, dz in places:
            rows += near_rows(dx, dz)
            first, second = near_weights(dx, dz)
            even += first
            odd += second
        mats = jnp.concatenate(
            [jnp.concatenate(even, axis=1), jnp.concatenate(odd, axis=1)], axis=0
        )
        return dot(jnp.concatenate(rows, axis=1), mats, NT)

    coarse_w[...] = jnp.zeros(coarse_w.shape, BF16)
    ch["last"][0].wait()
    near_acc[...] = near_product([(0, 0)])

    got_first(ch)
    got_first(on)
    got_first(mo)
    tw[0].wait()
    tw[1].start()
    local[8].wait()
    chunk = 8

    def build_coarse(u, carry):
        for t in range(chunk):
            for k in range(2):
                r = 2 * (chunk * u + t) + k
                x, y, z = r // (sizes[1] * sizes[2]), r // sizes[2] % sizes[1], r % sizes[2]
                value = coarse_raw[x, y, z]
                for s in range(2):
                    col = k * pts + s * lane
                    coarse_w[chunk * u + t, s * lane : s * lane + rank, col : col + rank] = value
        return carry

    lax.fori_loop(0, cells // 2 // chunk, build_coarse, 0)

    got_second(on)
    ch["last"][1].wait()
    near_acc[...] += near_product([(-1, 0), (1, 0)])
    tw[1].wait()
    tw[2].start()
    got_second(mo)
    got_edge(on)
    got_second(ch)
    got_edge(mo)
    got_edge(ch)
    tw[2].wait()

    group = 16

    def coarse_step(u, total):
        rows, mats = [], []
        for k in range(group):
            t = u * group + k
            for r in (2 * t, 2 * t + 1):
                x, y, z = r // (sizes[1] * sizes[2]), r // sizes[2] % sizes[1], r % sizes[2]
                rows.append(
                    two[
                        lax.rem(me[0] + x, sizes[0]),
                        lax.rem(me[1] + y, sizes[1]),
                        lax.rem(me[2] + z, sizes[2]),
                    ]
                )
            mats.append(coarse_w[t])
        return total + dot(jnp.concatenate(rows, axis=1), jnp.concatenate(mats, axis=1), NT)

    local_two = lax.fori_loop(
        0, cells // 2 // group, coarse_step, jnp.zeros((half, pts), F32)
    )

    on["last"][0].wait()

    def expand(ref, places):
        n = ref.shape[4]
        tiles = [
            jnp.concatenate(
                [ref[a, q // 2, b, q % 2].reshape(n * half, pts) for a, b in places], axis=0
            )
            for q in range(parts)
        ]
        whole = unpack(tiles)
        for k, (a, b) in enumerate(places):
            piece = whole[k * n * half : (k + 1) * n * half]
            ref[a, 1, b, 1] = piece.reshape(n, half, pts)

    expand(one, [(a, b) for a in range(one.shape[0]) for b in range(one.shape[2])])

    def boxes_of(ref):
        xs, px, ys, py, zs = ref.shape[:5]
        return ref.reshape(xs * px, ys * py, zs, half, pts)

    mom_box, one_box = boxes_of(mom), boxes_of(one)

    def far_window(ref, level, e, count):
        ox, oy, oz = (far_offsets[d, level, e] + 2 for d in range(3))
        planes = []
        for i in range(count[0]):
            x = lax.rem(ox + i, ref.shape[0]) if wrap(ref, count) else ox + i
            v = ref[x, pl.ds(oy, count[1]), pl.ds(oz, count[2])]
            planes.append(v.reshape(count[1] * count[2] * half, pts))
        return jnp.concatenate(planes, axis=0)

    def wrap(ref, count):
        return ref.shape[0] < count[0] + 4

    def far_product(ref, level, t, many, count):
        rows = [far_window(ref, level, 4 * t + k, count) for k in range(4 * many)]
        mats = [far_w[level, t + k] for k in range(many)]
        return dot(jnp.concatenate(rows, axis=1), jnp.concatenate(mats, axis=1), NT)

    one_acc[...] = jnp.zeros(one_acc.shape, F32)

    def far_one(t, carry):
        one_acc[...] += far_product(one_box, 1, 4 * t, 4, (hx, hy, hz))
        return carry

    lax.fori_loop(0, steps // 16, far_one, 0)

    rounded = local_two.astype(BF16)
    for number in range(8):
        rows = slice(number * half, (number + 1) * half)
        one_acc[rows, :] += dot(rounded, trans_w[number], NN)

    rounded = one_acc[...].astype(BF16)
    for number, (i, j, l) in enumerate(kids):
        value = dot(rounded, trans_w[number], NN)
        for n, (a, b, c) in enumerate(parents):
            box = ((2 * a + i) * by + 2 * b + j) * bz + 2 * c + l
            far_acc[box * half : (box + 1) * half, :] = value[n * half : (n + 1) * half]

    ch["last"][2].wait()
    near_acc[...] += near_product([(0, -1), (0, 1)])

    def expand_middle(u, carry):
        expand(mom, [(2 * u + i, b) for i in range(2) for b in range(1, 1 + hy)])
        return carry

    lax.fori_loop(0, mom.shape[0] // 2, expand_middle, 0)
    mo["last"][0].wait()

    def expand_outer(u, carry):
        expand(mom, [(2 * u + i, b) for i in range(2) for b in (0, 1 + hy)])
        return carry

    lax.fori_loop(0, mom.shape[0] // 2, expand_outer, 0)

    def far_zero(t, carry):
        far_acc[...] += far_product(mom_box, 0, 2 * t, 2, (bx, by, bz))
        return carry

    lax.fori_loop(0, steps // 8, far_zero, 0)

    ch["last"][3].wait()
    near_acc[...] += near_product([(-1, -1), (-1, 1)])
    near_acc[...] += near_product([(1, -1), (1, 1)])

    def finish(x, carry):
        span = by * bz * half
        rows = far_acc[pl.ds(pl.multiple_of(x * span, span), span), :].astype(BF16)
        value = dot(rows, basis_w[...], NN)
        for b in range(by * bz):
            y, z = b // bz, b % bz
            live = (lanes < counts[x, y, z]).astype(F32)
            live = jnp.concatenate([live, live], axis=0)
            far = jnp.concatenate(
                [
                    value[b * half : (b + 1) * half, 0:pts],
                    value[b * half : (b + 1) * half, pts : 2 * pts],
                ],
                axis=0,
            )
            at = pl.multiple_of(((y // 2 * bx + x) * bz + z) * rhs, rhs)
            col = y % 2 * pts
            out[x, y, z] = (near_acc[pl.ds(at, rhs), col : col + pts] + far) * live
        return carry

    lax.fori_loop(0, bx, finish, 0)

    drain(send_sem.at[0], sent[0])


def body(
    sizes,
    charges,
    counts,
    near_offsets,
    near_blocks,
    leaf_basis,
    transfer,
    far_offsets,
    coupling,
    coarse_coupling,
):
    bx, by, bz, rhs, pts = charges.shape
    half = rhs // 2
    stencil = near_offsets.shape[0]
    boxes = bx * by * bz
    hx, hy, hz = bx // 2, by // 2, bz // 2
    one_x = hx + 2 if sizes[0] * hx == hx + 2 else hx + 4
    levels, steps = coupling.shape[:2]
    rank = leaf_basis.shape[0]
    parts = rank // (pts // 2 - rank)
    cells = sizes[0] * sizes[1] * sizes[2]
    vmem = pl.BlockSpec(memory_space=pltpu.VMEM)
    hbm = pl.BlockSpec(memory_space=pl.ANY)
    return pl.pallas_call(
        functools.partial(kernel, sizes),
        out_shape=pltpu.VMEM(charges.shape, F32),
        in_specs=[hbm] * 9,
        out_specs=vmem,
        scratch_shapes=[
            pltpu.SMEM((3, stencil), jnp.int32),
            pltpu.SMEM(counts.shape, jnp.int32),
            pltpu.SMEM((3,) + far_offsets.shape[:2], jnp.int32),
            pltpu.VMEM(charges.shape, BF16),
            pltpu.VMEM(leaf_basis.shape, BF16),
            pltpu.VMEM(transfer.shape, BF16),
            pltpu.VMEM((bx + 2, by + 2, bz + 2, rhs, pts), BF16),
            pltpu.VMEM((hx + 2, 2, hy + 2, 2, bz + 4, half, pts), BF16),
            pltpu.VMEM((one_x // 2, 2, hy // 2 + 2, 2, hz + 4, half, pts), BF16),
            pltpu.VMEM(tuple(sizes) + (half, pts), BF16),
            pltpu.VMEM(near_blocks.shape, BF16),
            pltpu.VMEM(coupling.shape, BF16),
            pltpu.VMEM(coarse_coupling.shape, BF16),
            pltpu.VMEM((levels, steps // 4, pts, 4 * pts), BF16),
            pltpu.VMEM((cells // 2, pts, 2 * pts), BF16),
            pltpu.VMEM((8, pts, pts), BF16),
            pltpu.VMEM((pts, 2 * pts), BF16),
            pltpu.VMEM((pts, parts * pts), BF16),
            pltpu.VMEM((boxes // 2 * rhs, 2 * pts), F32),
            pltpu.VMEM((boxes * half, pts), F32),
            pltpu.VMEM((hx * hy * hz * half, pts), F32),
            pltpu.VMEM((512, half, pts), BF16),
            pltpu.SMEM((9,), jnp.int32),
            pltpu.SemaphoreType.DMA((9,)),
            pltpu.SemaphoreType.DMA((1,)),
            pltpu.SemaphoreType.DMA((24,)),
        ],
        compiler_params=pltpu.CompilerParams(
            collective_id=0, has_side_effects=True, vmem_limit_bytes=56 * 1024 * 1024
        ),
    )(
        near_offsets.T,
        counts,
        far_offsets.transpose(2, 0, 1),
        charges,
        leaf_basis,
        transfer,
        near_blocks,
        coupling,
        coarse_coupling,
    )


def solution(mesh):
    sizes = tuple(mesh.shape[a] for a in AXES)
    in_specs = (
        P("gx", "gy", "gz", None, None),
        P("gx", "gy", "gz"),
        P(),
        P(),
        P(),
        P(),
        P(),
        P(),
        P(),
    )
    out_specs = P("gx", "gy", "gz", None, None)
    return jax.shard_map(
        functools.partial(body, sizes),
        mesh=mesh,
        in_specs=in_specs,
        out_specs=out_specs,
        check_vma=False,
    )
```

time: 44.6 us -> 37.6 us (0.84)
  Pallas kernels: 43.5 us -> 36.4 us
    pallas_call x1, Pallas kernels: 43.5 us -> 36.4 us  [body(): pl.pallas_call(functools.partial(kernel, sizes), out_shape=pltpu.VMEM(cha...]
where the time goes in v2:
time: 37.6 us; the launch traced here: 37.4 us
  Pallas kernels  36.4 us (97%)
  local copies, waits for them, and re-layouts  0.97 us (3%)
    pallas_call x1, Pallas kernels, body(): pl.pallas_call(functools.partial(kernel, sizes), out_shape=pltpu.VMEM(cha...  36.4 us
    unnamed x1, local copies, waits for them, and re-layouts  0.97 us

profile of v2, /device:TPU:1, one launch (start us, length us, event | category | flops | bytes accessed | tf_op | source)
XLA Modules:
  0.0 37.4 jit_solution(1465278109011997979)
XLA Ops:
  0.0 36.4 %shard_map.91 = f32[4,4,4,32,128]{4,3,2,1,0:T(8,128)S(1)} custom-call(s32[3,27]{1,0:T(4,128)} %bitcast.3, s32[4,4,4]{2,1,0:T(4,128)} %counts_hbm.1, s32[3,2,32]{2,1,0:T(2,128)} %bitcast.2, bf16[4,4,4,32,128]{4,3,2,1,0:T(8,128)(2,1)} %charges_hbm.1, bf16[48,128]{1,0:T(8,128)(2,1)} %basis_hbm.1, bf16[8,48,48]{2,1,0:T(8,128)(2,1)} %transfer_hbm.1, ...), custom_call_target="tpu_custom_call" | custom-call | tf_op jit(solution)/shard_map/pallas_call | solution.py:589
  36.4 1.0 %copy.11 = f32[4,4,4,32,128]{4,3,2,1,0:T(8,128)} copy(f32[4,4,4,32,128]{4,3,2,1,0:T(8,128)S(1)} %shard_map.91) | data formatting | bytes 2097152

commit v3 on v2

--- a/solution.py
+++ b/solution.py
@@ -171,9 +171,7 @@
 
         groups = {"A": [moves(Batch(), first, {}, side) for side in sides[first]]}
         groups["B"] = moves(Batch(), second, {})
-        groups["AB"] = Batch()
-        for a in sides[first]:
-            moves(groups["AB"], second, {first: a})
+        groups["AB"] = [moves(Batch(), second, {first: a}) for a in sides[first]]
         last = [Batch() for k in range(1 if packed else 4)]
         cuts = []
         for k, places in enumerate(
@@ -201,24 +199,23 @@
 
         groups["send"] = send
         groups["per"] = len(cuts[0][0].copies[: cuts[0][2]])
+        groups["unit"] = 2 if packed else 1
         return groups
 
-    def got_first(groups):
-        per_second = len(groups["B"].copies)
-        per_third = groups["per"]
-        for k, batch in enumerate(groups["A"]):
-            batch.wait()
-            groups["AB"].start(slice(k * per_second, (k + 1) * per_second))
-            groups["send"](1, k * per_third, (k + 1) * per_third)
-        sent[0] += groups["AB"].tiles
+    def got_first(groups, k):
+        groups["A"][k].wait()
+        per = groups["per"]
+        groups["AB"][k].start()
+        groups["send"](1, k * per, (k + 1) * per)
 
     def got_second(groups):
         groups["B"].wait()
         groups["send"](2)
 
-    def got_edge(groups):
-        groups["AB"].wait()
-        groups["send"](3)
+    def got_edge(groups, k):
+        groups["AB"][k].wait()
+        per = groups["per"] * (len(groups["B"].copies) // groups["unit"])
+        groups["send"](3, k * per, (k + 1) * per)
 
     ring = (2, 1, 0)
 
@@ -237,31 +234,8 @@
     third = rank // parts
     ch = halo(ext, (bx, by, bz), (1, 1, 1), (0, 2, 1), False)
     mo = halo(mom, (hx, hy, bz), (1, 1, 2), (2, 0, 1), True)
-    on = halo(one, (hx // 2, hy // 2, hz), (1, 1, 2), (0, 2, 1), True)
+    on = halo(one, (hx // 2, hy // 2, hz), (1, 1, 2), (2, 0, 1), True)
     tw = [gather(k) for k in range(3)]
-
-    local[2].wait()
-    local[3].wait()
-    basis_w[...] = jnp.zeros(basis_w.shape, BF16)
-    basis_w[0:rank, 0:pts] = basis[...]
-    basis_w[lane : lane + rank, pts : 2 * pts] = basis[...]
-    trans_w[...] = jnp.zeros(trans_w.shape, BF16)
-    for c in range(8):
-        trans_w[c, 0:rank, 0:rank] = transfer[c]
-        trans_w[c, lane : lane + rank, lane : lane + rank] = transfer[c]
-    far_w[...] = jnp.zeros(far_w.shape, BF16)
-    target = lax.broadcasted_iota(jnp.int32, (pts, pts), 0)
-    source = lax.broadcasted_iota(jnp.int32, (pts, pts), 1)
-    moved = jnp.where(source % lane >= rank, source - rank, -pts)
-    for q in range(parts):
-        hit = (target == moved + q * third).astype(F32).astype(BF16)
-        spread[:, q * pts : (q + 1) * pts] = hit
-
-    def pack(last):
-        return dot(last, spread[...], NN).astype(BF16)
-
-    def unpack(tiles):
-        return dot(jnp.concatenate(tiles, axis=1), spread[...], NT).astype(BF16)
 
     lanes = lax.broadcasted_iota(jnp.int32, (half, pts), 1)
     local[0].wait()
@@ -280,6 +254,23 @@
     for batch in ch["A"]:
         batch.start()
     ch["send"](0)
+
+    local[2].wait()
+    basis_w[...] = jnp.zeros(basis_w.shape, BF16)
+    basis_w[0:rank, 0:pts] = basis[...]
+    basis_w[lane : lane + rank, pts : 2 * pts] = basis[...]
+    target = lax.broadcasted_iota(jnp.int32, (pts, pts), 0)
+    source = lax.broadcasted_iota(jnp.int32, (pts, pts), 1)
+    moved = jnp.where(source % lane >= rank, source - rank, -pts)
+    for q in range(parts):
+        hit = (target == moved + q * third).astype(F32).astype(BF16)
+        spread[:, q * pts : (q + 1) * pts] = hit
+
+    def pack(last):
+        return dot(last, spread[...], NN).astype(BF16)
+
+    def unpack(tiles):
+        return dot(jnp.concatenate(tiles, axis=1), spread[...], NT).astype(BF16)
 
     values = []
     for x in range(bx):
@@ -299,9 +290,12 @@
     for batch in mo["A"]:
         batch.start()
     mo["send"](0)
-    mo["B"].start()
-    ch["B"].start()
-
+
+    local[3].wait()
+    trans_w[...] = jnp.zeros(trans_w.shape, BF16)
+    for c in range(8):
+        trans_w[c, 0:rank, 0:rank] = transfer[c]
+        trans_w[c, lane : lane + rank, lane : lane + rank] = transfer[c]
     parents = [(a, b, c) for a in range(hx) for b in range(hy) for c in range(hz)]
     kids = [(i, j, l) for i in range(2) for j in range(2) for l in range(2)]
     total = jnp.zeros((len(parents) * half, pts), F32)
@@ -329,12 +323,14 @@
     for number in range(8):
         total = total + dot(value[number * half : (number + 1) * half], trans_w[number], NT)
     two[me[0], me[1], me[2]] = total.astype(BF16)
+    tw[0].start()
     for batch in on["A"]:
         batch.start()
-    tw[0].start()
     on["B"].start()
     on["send"](0)
 
+    far_w[...] = jnp.zeros(far_w.shape, BF16)
+    coarse_w[...] = jnp.zeros(coarse_w.shape, BF16)
     local[4].wait()
     local[5].wait()
     stencil = near_offsets.shape[1]
@@ -359,48 +355,63 @@
         return carry
 
     lax.fori_loop(0, steps // 8, build_far, 0)
+
+    blank = jnp.zeros((pts, pts), BF16)
+    pairs_y = by // 2
+    half_rows = bx * bz * rhs
+
+    def near_rows(places, j, ks):
+        return jnp.concatenate(
+            [
+                ext[pl.ds(1 + dx, bx), 2 * j + k, pl.ds(1 + dz, bz)].reshape(half_rows, pts)
+                for dx, dz in places
+                for k in ks
+            ],
+            axis=1,
+        )
+
+    def near_weights(places, ks, lag):
+        blocks = []
+        for dx, dz in places:
+            for k in ks:
+                if not 0 <= k - lag < 3:
+                    blocks.append(blank)
+                    continue
+                found = (inverse[(dx + 1) * 3 + k - lag] // 32 ** (dz + 1)) % 32
+                blocks.append(near_w[jnp.minimum(found, near_w.shape[0] - 1)])
+        return jnp.concatenate(blocks, axis=1)
+
+    def near_own(places, first=False):
+        for j in range(pairs_y):
+            ks = [k for k in range(4) if 0 <= 2 * j + k - 1 < by]
+            mats = jnp.concatenate([near_weights(places, ks, lag) for lag in range(2)], axis=0)
+            value = dot(near_rows(places, j, ks), mats, NT)
+            at = slice(j * half_rows, (j + 1) * half_rows)
+            near_acc[at, :] = value if first else near_acc[at, :] + value
+
+    def near_halo(places):
+        for j, k, lag in ((0, 0, 0), (pairs_y - 1, 3, 1)):
+            value = dot(near_rows(places, j, [k]), near_weights(places, [k], lag), NT)
+            at = slice(j * half_rows, (j + 1) * half_rows)
+            near_acc[at, lag * pts : (lag + 1) * pts] += value
+
     local[6].wait()
-
-    blank = jnp.zeros((pts, pts), BF16)
-
-    def near_rows(dx, dz):
-        columns = []
-        for k in range(4):
-            planes = [
-                ext[pl.ds(1 + dx, bx), 2 * j + k, pl.ds(1 + dz, bz)].reshape(bx * bz * rhs, pts)
-                for j in range(by // 2)
-            ]
-            columns.append(jnp.concatenate(planes, axis=0))
-        return columns
-
-    def near_weights(dx, dz):
-        blocks = []
-        for k in range(3):
-            found = (inverse[(dx + 1) * 3 + k] // 32 ** (dz + 1)) % 32
-            blocks.append(near_w[jnp.minimum(found, near_w.shape[0] - 1)])
-        return blocks + [blank], [blank] + blocks
-
-    def near_product(places):
-        rows, even, odd = [], [], []
-        for dx, dz in places:
-            rows += near_rows(dx, dz)
-            first, second = near_weights(dx, dz)
-            even += first
-            odd += second
-        mats = jnp.concatenate(
-            [jnp.concatenate(even, axis=1), jnp.concatenate(odd, axis=1)], axis=0
-        )
-        return dot(jnp.concatenate(rows, axis=1), mats, NT)
-
-    coarse_w[...] = jnp.zeros(coarse_w.shape, BF16)
-    ch["last"][0].wait()
-    near_acc[...] = near_product([(0, 0)])
-
-    got_first(ch)
-    got_first(on)
-    got_first(mo)
-    tw[0].wait()
-    tw[1].start()
+    near_own([(0, 0)], True)
+
+    def expand(ref, places):
+        n = ref.shape[4]
+        tiles = [
+            jnp.concatenate(
+                [ref[a, q // 2, b, q % 2].reshape(n * half, pts) for a, b in places], axis=0
+            )
+            for q in range(parts)
+        ]
+        whole = unpack(tiles)
+        for k, (a, b) in enumerate(places):
+            piece = whole[k * n * half : (k + 1) * n * half]
+            ref[a, 1, b, 1] = piece.reshape(n, half, pts)
+
+    ch["B"].start()
     local[8].wait()
     chunk = 8
 
@@ -417,16 +428,38 @@
 
     lax.fori_loop(0, cells // 2 // chunk, build_coarse, 0)
 
+    got_first(ch, 0)
+    mo["B"].start()
+    got_first(ch, 1)
+    near_own([(-1, 0), (1, 0)])
+    tw[0].wait()
+    tw[1].start()
+    got_first(on, 0)
+    got_first(on, 1)
     got_second(on)
+    got_first(mo, 0)
+    got_first(mo, 1)
+    ch["last"][0].wait()
     ch["last"][1].wait()
-    near_acc[...] += near_product([(-1, 0), (1, 0)])
+    near_halo([(0, 0), (-1, 0), (1, 0)])
     tw[1].wait()
     tw[2].start()
     got_second(mo)
-    got_edge(on)
     got_second(ch)
-    got_edge(mo)
-    got_edge(ch)
+    near_own([(0, -1), (0, 1)])
+    got_edge(mo, 0)
+    got_edge(on, 0)
+    got_edge(on, 1)
+    got_edge(ch, 0)
+    got_edge(ch, 1)
+    near_own([(-1, -1), (-1, 1)])
+    got_edge(mo, 1)
+    near_own([(1, -1), (1, 1)])
+    def expand_middle(u, carry):
+        expand(mom, [(2 * u + i, b) for i in range(2) for b in range(1, 1 + hy)])
+        return carry
+
+    lax.fori_loop(0, mom.shape[0] // 2, expand_middle, 0)
     tw[2].wait()
 
     group = 16
@@ -452,20 +485,6 @@
     )
 
     on["last"][0].wait()
-
-    def expand(ref, places):
-        n = ref.shape[4]
-        tiles = [
-            jnp.concatenate(
-                [ref[a, q // 2, b, q % 2].reshape(n * half, pts) for a, b in places], axis=0
-            )
-            for q in range(parts)
-        ]
-        whole = unpack(tiles)
-        for k, (a, b) in enumerate(places):
-            piece = whole[k * n * half : (k + 1) * n * half]
-            ref[a, 1, b, 1] = piece.reshape(n, half, pts)
-
     expand(one, [(a, b) for a in range(one.shape[0]) for b in range(one.shape[2])])
 
     def boxes_of(ref):
@@ -511,31 +530,19 @@
             box = ((2 * a + i) * by + 2 * b + j) * bz + 2 * c + l
             far_acc[box * half : (box + 1) * half, :] = value[n * half : (n + 1) * half]
 
+    mo["last"][0].wait()
+
+    expand(mom, [(a, b) for a in range(mom.shape[0]) for b in (0, 1 + hy)])
+
+    def far_zero(t, carry):
+        far_acc[...] += far_product(mom_box, 0, 4 * t, 4, (bx, by, bz))
+        return carry
+
+    lax.fori_loop(0, steps // 16, far_zero, 0)
+
+    ch["last"][3].wait()
     ch["last"][2].wait()
-    near_acc[...] += near_product([(0, -1), (0, 1)])
-
-    def expand_middle(u, carry):
-        expand(mom, [(2 * u + i, b) for i in range(2) for b in range(1, 1 + hy)])
-        return carry
-
-    lax.fori_loop(0, mom.shape[0] // 2, expand_middle, 0)
-    mo["last"][0].wait()
-
-    def expand_outer(u, carry):
-        expand(mom, [(2 * u + i, b) for i in range(2) for b in (0, 1 + hy)])
-        return carry
-
-    lax.fori_loop(0, mom.shape[0] // 2, expand_outer, 0)
-
-    def far_zero(t, carry):
-        far_acc[...] += far_product(mom_box, 0, 2 * t, 2, (bx, by, bz))
-        return carry
-
-    lax.fori_loop(0, steps // 8, far_zero, 0)
-
-    ch["last"][3].wait()
-    near_acc[...] += near_product([(-1, -1), (-1, 1)])
-    near_acc[...] += near_product([(1, -1), (1, 1)])
+    near_halo([(dx, dz) for dz in (-1, 1) for dx in (0, -1, 1)])
 
     def finish(x, carry):
         span = by * bz * half

time: 37.6 us -> 32.6 us (0.87)
  Pallas kernels: 36.4 us -> 31.5 us
    pallas_call x1, Pallas kernels: 36.4 us -> 31.5 us  [body(): pl.pallas_call(functools.partial(kernel, sizes), out_shape=pltpu.VMEM(cha...]
where the time goes in v3:
time: 32.6 us; the launch traced here: 32.4 us
  Pallas kernels  31.5 us (97%)
  local copies, waits for them, and re-layouts  0.97 us (3%)
    pallas_call x1, Pallas kernels, body(): pl.pallas_call(functools.partial(kernel, sizes), out_shape=pltpu.VMEM(cha...  31.5 us
    unnamed x1, local copies, waits for them, and re-layouts  0.97 us

profile of v3, /device:TPU:1, one launch (start us, length us, event | category | flops | bytes accessed | tf_op | source)
XLA Modules:
  0.0 32.4 jit_solution(17339630072225999067)
XLA Ops:
  0.0 31.5 %shard_map.91 = f32[4,4,4,32,128]{4,3,2,1,0:T(8,128)S(1)} custom-call(s32[3,27]{1,0:T(4,128)} %bitcast.3, s32[4,4,4]{2,1,0:T(4,128)} %counts_hbm.1, s32[3,2,32]{2,1,0:T(2,128)} %bitcast.2, bf16[4,4,4,32,128]{4,3,2,1,0:T(8,128)(2,1)} %charges_hbm.1, bf16[48,128]{1,0:T(8,128)(2,1)} %basis_hbm.1, bf16[8,48,48]{2,1,0:T(8,128)(2,1)} %transfer_hbm.1, ...), custom_call_target="tpu_custom_call" | custom-call | tf_op jit(solution)/shard_map/pallas_call | solution.py:596
  31.5 1.0 %copy.11 = f32[4,4,4,32,128]{4,3,2,1,0:T(8,128)} copy(f32[4,4,4,32,128]{4,3,2,1,0:T(8,128)S(1)} %shard_map.91) | data formatting | bytes 2097152

commit v4 on v3

--- a/solution.py
+++ b/solution.py
@@ -171,7 +171,9 @@
 
         groups = {"A": [moves(Batch(), first, {}, side) for side in sides[first]]}
         groups["B"] = moves(Batch(), second, {})
-        groups["AB"] = [moves(Batch(), second, {first: a}) for a in sides[first]]
+        groups["AB"] = [
+            [moves(Batch(), second, {first: a}, b) for b in sides[second]] for a in sides[first]
+        ]
         last = [Batch() for k in range(1 if packed else 4)]
         cuts = []
         for k, places in enumerate(
@@ -205,7 +207,8 @@
     def got_first(groups, k):
         groups["A"][k].wait()
         per = groups["per"]
-        groups["AB"][k].start()
+        for batch in groups["AB"][k]:
+            batch.start()
         groups["send"](1, k * per, (k + 1) * per)
 
     def got_second(groups):
@@ -213,9 +216,11 @@
         groups["send"](2)
 
     def got_edge(groups, k):
-        groups["AB"][k].wait()
-        per = groups["per"] * (len(groups["B"].copies) // groups["unit"])
-        groups["send"](3, k * per, (k + 1) * per)
+        per = groups["per"]
+        for n, batch in enumerate(groups["AB"][k]):
+            batch.wait()
+            n += k * len(groups["AB"][k])
+            groups["send"](3, n * per, (n + 1) * per)
 
     ring = (2, 1, 0)
 
@@ -434,8 +439,8 @@
     near_own([(-1, 0), (1, 0)])
     tw[0].wait()
     tw[1].start()
-    got_first(on, 0)
-    got_first(on, 1)
+    for k in range(len(on["A"])):
+        got_first(on, k)
     got_second(on)
     got_first(mo, 0)
     got_first(mo, 1)
@@ -448,12 +453,13 @@
     got_second(ch)
     near_own([(0, -1), (0, 1)])
     got_edge(mo, 0)
-    got_edge(on, 0)
-    got_edge(on, 1)
+    for k in range(len(on["A"])):
+        got_edge(on, k)
     got_edge(ch, 0)
     got_edge(ch, 1)
     near_own([(-1, -1), (-1, 1)])
     got_edge(mo, 1)
+
     near_own([(1, -1), (1, 1)])
     def expand_middle(u, carry):
         expand(mom, [(2 * u + i, b) for i in range(2) for b in range(1, 1 + hy)])
@@ -544,7 +550,7 @@
     ch["last"][2].wait()
     near_halo([(dx, dz) for dz in (-1, 1) for dx in (0, -1, 1)])
 
-    def finish(x, carry):
+    def finish_plane(x):
         span = by * bz * half
         rows = far_acc[pl.ds(pl.multiple_of(x * span, span), span), :].astype(BF16)
         value = dot(rows, basis_w[...], NN)
@@ -562,9 +568,13 @@
             at = pl.multiple_of(((y // 2 * bx + x) * bz + z) * rhs, rhs)
             col = y % 2 * pts
             out[x, y, z] = (near_acc[pl.ds(at, rhs), col : col + pts] + far) * live
+
+    def finish(t, carry):
+        for u in range(2):
+            finish_plane(2 * t + u)
         return carry
 
-    lax.fori_loop(0, bx, finish, 0)
+    lax.fori_loop(0, hx, finish, 0)
 
     drain(send_sem.at[0], sent[0])
 
@@ -624,7 +634,7 @@
             pltpu.SMEM((9,), jnp.int32),
             pltpu.SemaphoreType.DMA((9,)),
             pltpu.SemaphoreType.DMA((1,)),
-            pltpu.SemaphoreType.DMA((24,)),
+            pltpu.SemaphoreType.DMA((32,)),
         ],
         compiler_params=pltpu.CompilerParams(
             collective_id=0, has_side_effects=True, vmem_limit_bytes=56 * 1024 * 1024

time: 32.6 us -> 32.4 us (level)
  no operation moved by 1% of the time
where the time goes in v4:
time: 32.4 us; the launch traced here: 32.2 us
  Pallas kernels  31.2 us (96%)
  local copies, waits for them, and re-layouts  0.97 us (3%)
    pallas_call x1, Pallas kernels, body(): pl.pallas_call(functools.partial(kernel, sizes), out_shape=pltpu.VMEM(cha...  31.2 us
    unnamed x1, local copies, waits for them, and re-layouts  0.97 us

profile of v4, /device:TPU:1, one launch (start us, length us, event | category | flops | bytes accessed | tf_op | source)
XLA Modules:
  0.0 32.2 jit_solution(16686900553863919170)
XLA Ops:
  0.0 31.2 %shard_map.91 = f32[4,4,4,32,128]{4,3,2,1,0:T(8,128)S(1)} custom-call(s32[3,27]{1,0:T(4,128)} %bitcast.3, s32[4,4,4]{2,1,0:T(4,128)} %counts_hbm.1, s32[3,2,32]{2,1,0:T(2,128)} %bitcast.2, bf16[4,4,4,32,128]{4,3,2,1,0:T(8,128)(2,1)} %charges_hbm.1, bf16[48,128]{1,0:T(8,128)(2,1)} %basis_hbm.1, bf16[8,48,48]{2,1,0:T(8,128)(2,1)} %transfer_hbm.1, ...), custom_call_target="tpu_custom_call" | custom-call | tf_op jit(solution)/shard_map/pallas_call | solution.py:606
  31.2 1.0 %copy.11 = f32[4,4,4,32,128]{4,3,2,1,0:T(8,128)} copy(f32[4,4,4,32,128]{4,3,2,1,0:T(8,128)S(1)} %shard_map.91) | data formatting | bytes 2097152
